TPU v7x, 32 devices: a whole 2x2x4 slice. The times are simulated.
32 devices in a mesh: grp: 16 (over z, x, core), mode: 2 (over y).
Axes of the slice: x: 2, y: 2, z: 4, core: 2. Of those that a mesh axis runs over, the one named last changes fastest.
Arguments:
- probe: float32 [2, 8, 512, 512], P(None, 'mode'), may hold values from -3 to 3
- prev_direction: float32 [2, 8, 512, 512], P(None, 'mode'), may hold values from -0.6 to 0.6
- prev_norm: float32 [8], P('mode'), may hold values from 0.5 to 4
- object_tile: bfloat16 [2, 10240, 640], P(None, 'grp'), may hold values from -4 to 4
- offsets: int32 [32, 2], P('grp'), may hold values from 0 to 128
- amplitude: bfloat16 [32, 512, 512], P('grp'), may hold values from 0.5 to 3.5
Outputs:
- new_probe: float32 [2, 8, 512, 512], P(None, 'mode')
- new_direction: float32 [2, 8, 512, 512], P(None, 'mode')
- new_norm: float32 [8], P('mode')
All inputs are finite; a program needn't handle non-finite values.
Results may differ from a plain program's by a relative error of at most 0.0045.
Values sent between devices are 32-bit elements; how exact they have to be, the bound alone decides.
A program may use at most 128 MiB of HBM per device.

v0:
```python
import math

import jax
import jax.numpy as jnp
from jax import lax
from jax.sharding import PartitionSpec as P

N = 512


def tables(width, sign):
    index = jnp.arange(width, dtype=jnp.int32)
    product = index[:, None] * index[None, :] % width
    angle = -2.0 * math.pi / width * product.astype(jnp.float32)
    scale = 1.0 / math.sqrt(width)
    real_part = (jnp.cos(angle) * scale).astype(jnp.bfloat16)
    imag_part = (sign * jnp.sin(angle) * scale).astype(jnp.bfloat16)
    right = jnp.concatenate(
        [jnp.concatenate([real_part, imag_part], 1), jnp.concatenate([-imag_part, real_part], 1)], 0
    )
    left = jnp.concatenate(
        [jnp.concatenate([real_part, -imag_part], 1), jnp.concatenate([imag_part, real_part], 1)], 0
    )
    return (right, left)


def transform(real_in, imag_in, right, left):
    count, width = (real_in.shape[0], real_in.shape[1])
    joined = jnp.concatenate([real_in, imag_in], axis=2).reshape(count * width, 2 * width)
    half = jnp.dot(joined, right, preferred_element_type=jnp.float32)
    half = half.astype(jnp.bfloat16).reshape(count, width, 2 * width)
    stacked = jnp.concatenate([half[:, :, :width], half[:, :, width:]], axis=1)
    out = jnp.einsum("ab,mbc->mac", left, stacked, preferred_element_type=jnp.float32)
    return (out[:, :width], out[:, width:])


def finish(grad_re, grad_im, illum, total, probe_part, dir_part, prev_norm):
    denom = illum + total / (N * N)
    pre_re = grad_re / denom
    pre_im = grad_im / denom
    pixels = float(N * N)
    new_norm = jnp.sum(grad_re * pre_re + grad_im * pre_im, axis=(1, 2))
    new_norm = new_norm / pixels
    beta = (new_norm / prev_norm)[:, None, None]
    dir_re = pre_re + beta * dir_part[0]
    dir_im = pre_im + beta * dir_part[1]
    upper = jnp.sum(grad_re * dir_re + grad_im * dir_im, axis=(1, 2))
    lower = jnp.sum(illum * (dir_re * dir_re + dir_im * dir_im), axis=(1, 2))
    alpha = (upper / pixels / (lower / pixels + 1.0))[:, None, None]
    new_direction = jnp.stack([dir_re, dir_im])
    new_probe = jnp.stack([probe_part[0] + alpha * dir_re, probe_part[1] + alpha * dir_im])
    return (new_probe, new_direction, new_norm)


def on_device(probe, prev_direction, prev_norm, object_tile, offsets, amplitude):
    width = probe.shape[2]
    fwd_right, fwd_left = tables(width, 1.0)
    inv_right, inv_left = tables(width, -1.0)
    probe_re, probe_im = (probe[0], probe[1])
    local_modes = probe.shape[1]
    grad_re = jnp.zeros((local_modes, width, width), jnp.float32)
    grad_im = jnp.zeros((local_modes, width, width), jnp.float32)
    illum = jnp.zeros((width, width), jnp.float32)
    for index in range(amplitude.shape[0]):
        patch = lax.dynamic_slice(
            object_tile, (jnp.int32(0), offsets[index, 0], offsets[index, 1]), (2, width, width)
        ).astype(jnp.float32)
        obj_re, obj_im = (patch[0], patch[1])
        exit_re = (probe_re * obj_re - probe_im * obj_im).astype(jnp.bfloat16)
        exit_im = (probe_re * obj_im + probe_im * obj_re).astype(jnp.bfloat16)
        wave_re, wave_im = transform(exit_re, exit_im, fwd_right, fwd_left)
        local_sum = jnp.sum(wave_re * wave_re + wave_im * wave_im, axis=0)
        measured = amplitude[index].astype(jnp.float32)
        rows = lax.psum_scatter(local_sum, "mode", scatter_dimension=0, tiled=True)
        count = rows.shape[0]
        part = lax.dynamic_slice_in_dim(measured, lax.axis_index("mode") * count, count, 0)
        ratio = lax.all_gather(part / jnp.sqrt(rows + 1.0), "mode", axis=0, tiled=True)
        fixed_re = (ratio * wave_re).astype(jnp.bfloat16)
        fixed_im = (ratio * wave_im).astype(jnp.bfloat16)
        back_re, back_im = transform(fixed_re, fixed_im, inv_right, inv_left)
        diff_re = back_re - exit_re.astype(jnp.float32)
        diff_im = back_im - exit_im.astype(jnp.float32)
        grad_re = grad_re + obj_re * diff_re + obj_im * diff_im
        grad_im = grad_im + obj_re * diff_im - obj_im * diff_re
        illum = illum + obj_re * obj_re + obj_im * obj_im
    grad_re, grad_im, illum = lax.psum((grad_re, grad_im, illum), "grp")
    total = jnp.sum(illum)
    new_probe, new_direction, new_norm = finish(
        grad_re, grad_im, illum, total, probe, prev_direction, prev_norm
    )
    return (new_probe, new_direction, new_norm)


def solution(mesh):
    return jax.shard_map(
        on_device,
        mesh=mesh,
        in_specs=(
            P(None, "mode", None, None),
            P(None, "mode", None, None),
            P("mode"),
            P(None, "grp", None),
            P("grp", None),
            P("grp", None, None),
        ),
        out_specs=(P(None, "mode", None, None), P(None, "mode", None, None), P("mode")),
        check_vma=False,
    )
```

profile of v0, /device:TPU:0, one launch (start us, length us, event | category | flops | bytes accessed | tf_op | source)
XLA Modules:
  0.0 513.6 jit_solution(14685794393002363671)
XLA Ops:
  18.4 5.4 %multiply_convert_fusion.5 = (bf16[512,512]{1,0:T(8,128)(2,1)}, bf16[512,512]{1,0:T(8,128)(2,1)}) fusion(), kind=kLoop, calls=%fused_computation.118 | loop fusion | flops 4718592 | bytes 1048576 | tf_op jit(solution)/shard_map/convert_element_type | solution.py:17
  23.8 7.7 %fusion.97 = (f32[1,4,512,512]{3,2,1,0:T(8,128)}, f32[1,4,512,512]{3,2,1,0:T(8,128)}) fusion(f32[2,4,512,512]{3,2,1,0:T(8,128)} %param.6), kind=kLoop, calls=%fused_computation.144 | loop fusion | bytes 16777216 | tf_op jit(solution)/shard_map/slice | solution.py:51
  42.2 5.3 %fusion.5 = (bf16[2048,512]{1,0:T(8,128)(2,1)S(1)}, bf16[2048,512]{1,0:T(8,128)(2,1)S(1)}, bf16[2048,512]{1,0:T(8,128)(2,1)}, bf16[2048,512]{1,0:T(8,128)(2,1)}) fusion(f32[1,4,512,512]{3,2,1,0:T(8,128)S(1)} %copy-done.3, f32[1,4,512,512]{3,2,1,0:T(8,128)S(1)} %copy-done.4, f32[512,512]{1,0:T(8,128)S(1)} %get-tuple-element.46, ...), kind=kLoop, calls=%fused_computation.15 | loop fusion | flops 16777216 | bytes 20971520 | tf_op jit(solution)/shard_map/convert_element_type | solution.py:69
  63.2 7.5 %fusion.53 = f32[4,1024,512]{1,2,0:T(8,128)S(1)} fusion(bf16[4,512,512]{1,2,0:T(8,128)(2,1)} %copy.96, bf16[4,512,512]{1,2,0:T(8,128)(2,1)} %copy.95, bf16[512,512]{1,0:T(8,128)(2,1)} %get-tuple-element.62, bf16[512,512]{1,0:T(8,128)(2,1)} %get-tuple-element.61, bf16[512,512]{1,0:T(8,128)(2,1)} %fusion.83), kind=kOutput, calls=%fused_computation.96 | convolution fusion | flops 4311744512 | bytes 14155776 | tf_op jit(solution)/shard_map/ab,mbc->mac/dot_general | solution.py:33
  76.4 7.3 %fusion.47 = bf16[2048,1024]{1,0:T(8,128)(2,1)S(1)} fusion(bf16[2048,512]{1,0:T(8,128)(2,1)} %get-tuple-element.33, bf16[2048,512]{1,0:T(8,128)(2,1)} %get-tuple-element.34, bf16[512,512]{1,0:T(8,128)(2,1)} %get-tuple-element.62, bf16[512,512]{1,0:T(8,128)(2,1)} %fusion.83, bf16[512,512]{1,0:T(8,128)(2,1)} %get-tuple-element.61), kind=kOutput, calls=%fused_computation.84 | convolution fusion | flops 4313841664 | bytes 9961472 | tf_op jit(solution)/shard_map/dot_general | solution.py:30
  94.5 7.5 %fusion.59 = f32[4,1024,512]{1,2,0:T(8,128)S(1)} fusion(bf16[4,512,512]{1,2,0:T(8,128)(2,1)} %copy.92, bf16[4,512,512]{1,2,0:T(8,128)(2,1)} %copy.91, bf16[512,512]{1,0:T(8,128)(2,1)} %get-tuple-element.62, bf16[512,512]{1,0:T(8,128)(2,1)} %get-tuple-element.61, bf16[512,512]{1,0:T(8,128)(2,1)} %fusion.83), kind=kOutput, calls=%fused_computation.98 | convolution fusion | flops 4311744512 | bytes 14155776 | tf_op jit(solution)/shard_map/ab,mbc->mac/dot_general | solution.py:33
  128.9 5.4 %copy.90 = f32[1,4,512,512]{2,3,1,0:T(8,128)} copy(f32[1,4,512,512]{3,2,1,0:T(8,128)} %get-tuple-element.36) | data formatting | bytes 8388608
  161.1 6.5 %copy.80 = bf16[4,512,1024]{2,1,0:T(8,128)(2,1)} copy(bf16[4,512,1024]{1,2,0:T(8,128)(2,1)} %pad_maximum_fusion.3) | data formatting | bytes 8388608 | tf_op jit(solution)/shard_map/concatenate | solution.py:29
  167.6 13.5 %convolution_convert_fusion = bf16[2048,1024]{1,0:T(8,128)(2,1)S(1)} fusion(bf16[2048,1024]{1,0:T(8,128)(2,1)} %bitcast.188, bf16[512,512]{1,0:T(8,128)(2,1)S(1)} %copy-done.21, bf16[512,512]{1,0:T(8,128)(2,1)S(1)} %fusion.84, bf16[512,512]{1,0:T(8,128)(2,1)S(1)} %copy-done.24), kind=kOutput, calls=%fused_computation.85 | convolution fusion | flops 4305453056 | bytes 9961472 | tf_op jit(solution)/shard_map/dot_general | solution.py:30
  196.7 6.2 %copy.70 = bf16[4,512,1024]{2,1,0:T(8,128)(2,1)} copy(bf16[4,512,1024]{1,2,0:T(8,128)(2,1)} %pad_maximum_fusion.2) | data formatting | bytes 8388608 | tf_op jit(solution)/shard_map/concatenate | solution.py:29
  203.0 13.5 %convolution_convert_fusion.1 = bf16[2048,1024]{1,0:T(8,128)(2,1)S(1)} fusion(bf16[2048,1024]{1,0:T(8,128)(2,1)} %bitcast.189, bf16[512,512]{1,0:T(8,128)(2,1)S(1)} %copy-done.21, bf16[512,512]{1,0:T(8,128)(2,1)S(1)} %fusion.84, bf16[512,512]{1,0:T(8,128)(2,1)S(1)} %copy-done.25), kind=kOutput, calls=%fused_computation.86 | convolution fusion | flops 4305453056 | bytes 9961472 | tf_op jit(solution)/shard_map/dot_general | solution.py:30
  224.9 10.4 %fusion.50 = f32[4,1024,512]{1,2,0:T(8,128)} fusion(bf16[4,512,512]{1,2,0:T(8,128)(2,1)} %copy.98, bf16[4,512,512]{1,2,0:T(8,128)(2,1)} %copy.97, bf16[512,512]{1,0:T(8,128)(2,1)S(1)} %copy-done.21, bf16[512,512]{1,0:T(8,128)(2,1)} %multiply_convert_fusion.4, bf16[512,512]{1,0:T(8,128)(2,1)S(1)} %fusion.84), kind=kOutput, calls=%fused_computation.95 | convolution fusion | flops 4311744512 | bytes 14155776 | tf_op jit(solution)/shard_map/ab,mbc->mac/dot_general | solution.py:33
  235.4 8.3 %fusion.56 = f32[4,1024,512]{1,2,0:T(8,128)} fusion(bf16[4,512,512]{1,2,0:T(8,128)(2,1)S(1)} %copy-done.18, bf16[4,512,512]{1,2,0:T(8,128)(2,1)S(1)} %copy-done.17, bf16[512,512]{1,0:T(8,128)(2,1)S(1)} %copy-done.21, bf16[512,512]{1,0:T(8,128)(2,1)S(1)} %copy-done.26, bf16[512,512]{1,0:T(8,128)(2,1)S(1)} %fusion.84), kind=kOutput, calls=%fused_computation.97 | convolution fusion | flops 4311744512 | bytes 14155776 | tf_op jit(solution)/shard_map/ab,mbc->mac/dot_general | solution.py:33
  243.8 10.0 %multiply_add_fusion = (f32[4,512,512]{1,2,0:T(8,128)}, f32[4,512,512]{1,2,0:T(8,128)}) fusion(f32[4,1024,512]{1,2,0:T(8,128)} %fusion.56, f32[4,1024,512]{1,2,0:T(8,128)} %fusion.50, f32[512,512]{0,1:T(8,128)S(1)} %copy-done.14, f32[512,512]{0,1:T(8,128)S(1)} %copy-done.13, f32[512,512]{0,1:T(8,128)S(1)} %copy-done.15, f32[512,512]{0,1:T(8,128)S(1)} %copy-done.16, ...), kind=kLoop, calls=%fused_computation.76 | loop fusion | flops 39845888 | bytes 37748736 | tf_op jit(solution)/shard_map/add | solution.py:83
  253.9 8.3 %fusion.96 = (f32[1,4,512,512]{3,2,1,0:T(8,128)}, f32[1,4,512,512]{3,2,1,0:T(8,128)}) fusion(f32[2,4,512,512]{3,2,1,0:T(8,128)} %param.7), kind=kLoop, calls=%fused_computation.143 | loop fusion | bytes 16777216 | tf_op jit(solution)/shard_map/slice | solution.py:46
  262.1 5.3 %copy.100 = f32[1,4,512,512]{2,3,1,0:T(8,128)} copy(f32[1,4,512,512]{3,2,1,0:T(8,128)} %get-tuple-element.31) | data formatting | bytes 8388608
  267.5 5.5 %copy.99 = f32[1,4,512,512]{2,3,1,0:T(8,128)} copy(f32[1,4,512,512]{3,2,1,0:T(8,128)} %get-tuple-element.32) | data formatting | bytes 8388608
  272.9 165.7 %all-reduce.3.cloned.1.call-done = (f32[4,512,512]{1,2,0:T(8,128)}, f32[4,512,512]{1,2,0:T(8,128)}, f32[512,512]{1,0:T(8,128)}) async-done(((f32[4,512,512]{1,2,0:T(8,128)}, f32[4,512,512]{1,2,0:T(8,128)}, f32[512,512]{1,0:T(8,128)}), (f32[4,512,512]{1,2,0:T(8,128)}, f32[4,512,512]{1,2,0:T(8,128)}, f32[512,512]{1,0:T(8,128)})) %all-reduce.3.cloned.1.call-update) | async-done | bytes 9437200 | tf_op jit(solution)/shard_map/psum | solution.py:86
  452.7 8.6 %add_reduce_fusion = (f32[4]{0:T(128)S(1)}, f32[4]{0:T(128)S(1)}, f32[4,512,512]{1,2,0:T(8,128)}, f32[4,512,512]{1,2,0:T(8,128)}) fusion(f32[4,512,512]{1,2,0:T(8,128)S(1)} %copy-done.8, f32[4,512,512]{1,2,0:T(8,128)S(1)} %copy-done.9, f32[512,512]{0,1:T(8,128)S(1)} %copy.86, f32[1,4,512,512]{2,3,1,0:T(8,128)} %copy.99, f32[4]{0:T(128)S(1)} %get-tuple-element.19, ...), kind=kLoop, calls=%fused_computation.73 | loop fusion | flops 15728632 | bytes 27263024 | tf_op jit(solution)/shard_map/reduce_sum | solution.py:47
  461.3 10.2 %fusion.43 = (f32[1,4,512,512]{2,3,1,0:T(8,128)}, f32[1,4,512,512]{2,3,1,0:T(8,128)}) fusion(f32[1,4,512,512]{2,3,1,0:T(8,128)S(1)} %copy-done.1, f32[4,512,512]{1,2,0:T(8,128)} %get-tuple-element.17, f32[4]{0:T(128)S(1)} %add_divide_fusion, f32[4,512,512]{1,2,0:T(8,128)} %get-tuple-element.18, f32[1,4,512,512]{2,3,1,0:T(8,128)} %copy.90), kind=kLoop, calls=%fused_computation.71 | loop fusion | flops 4194304 | bytes 25165840 | tf_op jit(solution)/shard_map/stack | solution.py:51
  471.6 7.8 %pad_maximum_fusion = f32[2,4,512,512]{2,3,1,0:T(8,128)} fusion(f32[1,4,512,512]{2,3,1,0:T(8,128)} %get-tuple-element.58, f32[1,4,512,512]{2,3,1,0:T(8,128)} %get-tuple-element.57), kind=kLoop, calls=%fused_computation | loop fusion | flops 2097152 | bytes 16777216 | tf_op jit(solution)/shard_map/stack | solution.py:51
  479.4 9.9 %copy.87 = f32[2,4,512,512]{3,2,1,0:T(8,128)} copy(f32[2,4,512,512]{2,3,1,0:T(8,128)} %pad_maximum_fusion) | data formatting | bytes 16777216
  489.3 7.7 %pad_maximum_fusion.1 = f32[2,4,512,512]{2,3,1,0:T(8,128)} fusion(f32[1,4,512,512]{2,3,1,0:T(8,128)} %bitcast.183, f32[1,4,512,512]{2,3,1,0:T(8,128)} %bitcast.182), kind=kLoop, calls=%fused_computation.1 | loop fusion | flops 2097152 | bytes 16777216 | tf_op jit(solution)/shard_map/stack | solution.py:50
  497.0 9.9 %copy.88 = f32[2,4,512,512]{3,2,1,0:T(8,128)} copy(f32[2,4,512,512]{2,3,1,0:T(8,128)} %pad_maximum_fusion.1) | data formatting | bytes 16777216
  (115 shorter events, 137.4 us)
Async XLA Ops:
  7.2 105.4 %reduce-scatter.5.cloned.1.call-start = ((), (), s32[]{:S(2)}) async-start(), calls=%async_computation.4 | async-start | bytes 1572864 | tf_op jit(solution)/shard_map/reduce_scatter | solution.py:74
  38.2 9.4 %copy-start.10 = (f32[512,512]{1,0:T(8,128)}, f32[512,512]{1,0:T(8,128)S(1)}, u32[]{:S(2)}) copy-start(f32[512,512]{1,0:T(8,128)S(1)} %get-tuple-element.59) | copy-start | bytes 3145732
  38.2 9.4 %copy-start.11 = (f32[512,512]{1,0:T(8,128)}, f32[512,512]{1,0:T(8,128)S(1)}, u32[]{:S(2)}) copy-start(f32[512,512]{1,0:T(8,128)S(1)} %get-tuple-element.46) | copy-start | bytes 3145732
  38.2 9.4 %copy-start.12 = (f32[512,512]{1,0:T(8,128)}, f32[512,512]{1,0:T(8,128)S(1)}, u32[]{:S(2)}) copy-start(f32[512,512]{1,0:T(8,128)S(1)} %get-tuple-element.45) | copy-start | bytes 3145732
  42.2 5.3 %copy-start.23 = (bf16[512,512]{1,0:T(8,128)(2,1)S(1)}, bf16[512,512]{1,0:T(8,128)(2,1)}, u32[]{:S(2)}) copy-start(bf16[512,512]{1,0:T(8,128)(2,1)} %get-tuple-element.61) | copy-start | bytes 1572868
  76.3 69.9 %reduce-scatter.3.cloned.1.call-start = ((), (), s32[]{:S(2)}) async-start(), calls=%async_computation.2 | async-start | bytes 1572864 | tf_op jit(solution)/shard_map/reduce_scatter | solution.py:74
  107.6 46.3 %all-gather.5.cloned.1.call-start = ((), (), s32[]{:S(2)}) async-start(), calls=%async_computation.5 | async-start | bytes 1572864 | tf_op jit(solution)/shard_map/all_gather | solution.py:77
  114.6 74.8 %all-gather.3.cloned.1.call-start = ((), (), s32[]{:S(2)}) async-start(), calls=%async_computation.3 | async-start | bytes 1572864 | tf_op jit(solution)/shard_map/all_gather | solution.py:77
  128.9 5.4 %copy-start.19 = (bf16[1,512,512]{2,1,0:T(8,128)(2,1)S(1)}, bf16[1,512,512]{2,1,0:T(8,128)(2,1)}, u32[]{:S(2)}) copy-start(bf16[1,512,512]{2,1,0:T(8,128)(2,1)} %get-tuple-element.52) | copy-start | bytes 1572868
  148.2 290.5 %all-reduce.3.cloned.1.call-start = ((), (), s32[]{:S(2)}) async-start(), calls=%async_computation.6 | async-start | bytes 18874368 | tf_op jit(solution)/shard_map/psum | solution.py:86
  161.1 6.5 %copy-start.21 = (bf16[512,512]{1,0:T(8,128)(2,1)S(1)}, bf16[512,512]{1,0:T(8,128)(2,1)}, u32[]{:S(2)}) copy-start(bf16[512,512]{1,0:T(8,128)(2,1)} %get-tuple-element.62) | copy-start | bytes 1572868
  161.1 6.5 %copy-start.24 = (bf16[512,512]{1,0:T(8,128)(2,1)S(1)}, bf16[512,512]{1,0:T(8,128)(2,1)}, u32[]{:S(2)}) copy-start(bf16[512,512]{1,0:T(8,128)(2,1)} %multiply_convert_fusion.4) | copy-start | bytes 1572868
  196.7 6.3 %copy-start.25 = (bf16[512,512]{1,0:T(8,128)(2,1)S(1)}, bf16[512,512]{1,0:T(8,128)(2,1)}, u32[]{:S(2)}) copy-start(bf16[512,512]{1,0:T(8,128)(2,1)} %multiply_convert_fusion.4) | copy-start | bytes 1572868
  224.9 10.4 %copy-start.17 = (bf16[4,512,512]{1,2,0:T(8,128)(2,1)S(1)}, bf16[4,512,512]{1,2,0:T(8,128)(2,1)}, u32[]{:S(2)}) copy-start(bf16[4,512,512]{1,2,0:T(8,128)(2,1)} %copy.93) | copy-start | bytes 6291460
  224.9 10.4 %copy-start.18 = (bf16[4,512,512]{1,2,0:T(8,128)(2,1)S(1)}, bf16[4,512,512]{1,2,0:T(8,128)(2,1)}, u32[]{:S(2)}) copy-start(bf16[4,512,512]{1,2,0:T(8,128)(2,1)} %copy.94) | copy-start | bytes 6291460
  224.9 10.4 %copy-start.26 = (bf16[512,512]{1,0:T(8,128)(2,1)S(1)}, bf16[512,512]{1,0:T(8,128)(2,1)}, u32[]{:S(2)}) copy-start(bf16[512,512]{1,0:T(8,128)(2,1)} %multiply_convert_fusion.4) | copy-start | bytes 1572868
  235.4 8.4 %copy-start = (f32[1,4,512,512]{2,3,1,0:T(8,128)S(1)}, f32[1,4,512,512]{2,3,1,0:T(8,128)}, u32[]{:S(2)}) copy-start(f32[1,4,512,512]{2,3,1,0:T(8,128)} %copy.89) | copy-start | bytes 12582916
  235.4 8.4 %copy-start.2 = (f32[1,4,512,512]{2,3,1,0:T(8,128)S(1)}, f32[1,4,512,512]{2,3,1,0:T(8,128)}, u32[]{:S(2)}) copy-start(f32[1,4,512,512]{2,3,1,0:T(8,128)} %copy.90) | copy-start | bytes 12582916
  235.4 8.4 %copy-start.13 = (f32[512,512]{0,1:T(8,128)S(1)}, f32[512,512]{0,1:T(8,128)}, u32[]{:S(2)}) copy-start(f32[512,512]{0,1:T(8,128)} %copy.73) | copy-start | bytes 3145732
  235.4 8.4 %copy-start.14 = (f32[512,512]{0,1:T(8,128)S(1)}, f32[512,512]{0,1:T(8,128)}, u32[]{:S(2)}) copy-start(f32[512,512]{0,1:T(8,128)} %copy.75) | copy-start | bytes 3145732
  235.4 8.4 %copy-start.15 = (f32[512,512]{0,1:T(8,128)S(1)}, f32[512,512]{0,1:T(8,128)}, u32[]{:S(2)}) copy-start(f32[512,512]{0,1:T(8,128)} %copy.65) | copy-start | bytes 3145732
  235.4 8.4 %copy-start.16 = (f32[512,512]{0,1:T(8,128)S(1)}, f32[512,512]{0,1:T(8,128)}, u32[]{:S(2)}) copy-start(f32[512,512]{0,1:T(8,128)} %copy.60) | copy-start | bytes 3145732
  446.8 5.9 %copy-start.9 = (f32[4,512,512]{1,2,0:T(8,128)S(1)}, f32[4,512,512]{1,2,0:T(8,128)}, u32[]{:S(2)}) copy-start(f32[4,512,512]{1,2,0:T(8,128)} %get-tuple-element.15) | copy-start | bytes 12582916
  452.7 8.6 %copy-start.1 = (f32[1,4,512,512]{2,3,1,0:T(8,128)S(1)}, f32[1,4,512,512]{2,3,1,0:T(8,128)}, u32[]{:S(2)}) copy-start(f32[1,4,512,512]{2,3,1,0:T(8,128)} %copy.89) | copy-start | bytes 12582916
  (9 other events, 38.4 us)
Sparse Core Ops, SparseCore 0:
  76.4 23.1 reduce-scatter.4
  107.7 23.1 reduce-scatter.2
  132.4 21.3 all-gather.4
  155.2 21.1 all-gather.2
  254.0 184.6 all-reduce.2
where the time goes:
time: 524 us; the launch traced here: 514 us
  waiting for transfers between devices  171 us (33%)
  local copies, waits for them, and re-layouts  139 us (27%)
  other arithmetic  108 us (21%)
  matrix products  72.5 us (14%)
  between operations  22.7 us (4%)
    psum x1, waiting for transfers between devices, on_device(): grad_re, grad_im, illum = lax.psum((grad_re, grad_im, illum), 'grp')  166 us
    unnamed x70, local copies, waits for them, and re-layouts  83.9 us
    dot_general x4, matrix products, transform(): half = jnp.dot(joined, right, preferred_element_type=jnp.float32)  38.8 us
    dot_general x4, matrix products, transform(): jnp.einsum('ab,mbc->mac', left, stacked, preferred_element_type=jnp.float32)  33.7 us
    another operation x2, other arithmetic, finish(): jnp.stack([probe_part[0] + alpha * dir_re, probe_part[1] + alpha * dir_im])  18.1 us
    concatenate x2, local copies, waits for them, and re-layouts, transform(): jnp.concatenate([real_in, imag_in], axis=2)  12.7 us
  transfers between devices with their start and end apart: 5, of which 2 were waited for; matrix products, arithmetic and copies ran while one was open for 24% of the time, Pallas kernels for 0%

commit v1 on v0

v1 whole, which is shorter than its diff:
```python
import functools
import math

import jax
import jax.numpy as jnp
from jax import lax
from jax.experimental import pallas as pl
from jax.experimental.pallas import tpu as pltpu
from jax.sharding import PartitionSpec as P

VMEM_LIMIT = 60 * 1024 * 1024
TILE = 256


def base_table(width):
    index = jnp.arange(width, dtype=jnp.int32)
    product = index[:, None] * index[None, :] % width
    angle = -2.0 * math.pi / width * product.astype(jnp.float32)
    scale = 1.0 / math.sqrt(width)
    real_part = (jnp.cos(angle) * scale).astype(jnp.bfloat16)
    imag_part = (jnp.sin(angle) * scale).astype(jnp.bfloat16)
    return jnp.stack([real_part, imag_part])


def build_pair(base_ref, plus, minus):
    width = base_ref.shape[1]
    cosine, sine = base_ref[0], base_ref[1]
    for ref, sign in ((plus, 1), (minus, -1)):
        ref[:width, :width] = cosine
        ref[width:, width:] = cosine
        ref[:width, width:] = sine if sign > 0 else -sine
        ref[width:, :width] = -sine if sign > 0 else sine


def transform(joined, stacked, right, left, emit):
    width = joined.shape[0]
    tile = min(TILE, width)

    def first(step, carry):
        at = pl.multiple_of(step * tile, tile)
        half = jnp.dot(joined[pl.ds(at, tile), :], right[...], preferred_element_type=jnp.float32)
        half = half.astype(jnp.bfloat16)
        stacked[pl.ds(at, tile), :] = half[:, :width]
        stacked[pl.ds(at + width, tile), :] = half[:, width:]
        return carry

    def second(step, carry):
        at = pl.multiple_of(step * tile, tile)
        rows = pl.ds(at, tile)
        real = jnp.dot(left[rows, :], stacked[...], preferred_element_type=jnp.float32)
        imag = jnp.dot(left[pl.ds(at + width, tile), :], stacked[...], preferred_element_type=jnp.float32)
        emit(rows, real, imag)
        return carry

    lax.fori_loop(0, width // tile, first, 0)
    lax.fori_loop(0, width // tile, second, 0)


def forward_kernel(base_ref, probe_ref, patch_ref, wave_ref, exit_ref, sum_ref, plus, minus, joined, stacked):
    mode = pl.program_id(0)
    width = sum_ref.shape[0]
    tile = 64

    @pl.when(mode == 0)
    def _():
        build_pair(base_ref, plus, minus)
        sum_ref[...] = jnp.zeros_like(sum_ref)

    def leave(step, carry):
        rows = pl.ds(pl.multiple_of(step * tile, tile), tile)
        obj_re = patch_ref[0, rows, :].astype(jnp.float32)
        obj_im = patch_ref[1, rows, :].astype(jnp.float32)
        pro_re, pro_im = probe_ref[0, 0, rows, :], probe_ref[1, 0, rows, :]
        exit_re = (pro_re * obj_re - pro_im * obj_im).astype(jnp.bfloat16)
        exit_im = (pro_re * obj_im + pro_im * obj_re).astype(jnp.bfloat16)
        joined[rows, :width] = exit_re
        joined[rows, width:] = exit_im
        exit_ref[0, 0, rows, :] = exit_re
        exit_ref[0, 1, rows, :] = exit_im
        return carry

    lax.fori_loop(0, width // tile, leave, 0)

    def emit(rows, real, imag):
        wave_ref[0, 0, rows, :] = real
        wave_ref[0, 1, rows, :] = imag
        sum_ref[rows, :] += real * real + imag * imag

    transform(joined, stacked, plus, minus, emit)


def backward_kernel(first, base_ref, total_ref, amp_ref, wave_ref, exit_ref, patch_ref, *rest):
    if first:
        grad_in, (grad_ref, plus, minus, joined, stacked, ratio) = None, rest
    else:
        grad_in, grad_ref, plus, minus, joined, stacked, ratio = rest
    width = total_ref.shape[0]
    tile = 64

    @pl.when(pl.program_id(0) == 0)
    def _():
        build_pair(base_ref, plus, minus)

        def scale(step, carry):
            rows = pl.ds(pl.multiple_of(step * tile, tile), tile)
            ratio[rows, :] = amp_ref[0, rows, :].astype(jnp.float32) / jnp.sqrt(total_ref[rows, :] + 1.0)
            return carry

        lax.fori_loop(0, width // tile, scale, 0)

    def fix(step, carry):
        rows = pl.ds(pl.multiple_of(step * tile, tile), tile)
        joined[rows, :width] = (ratio[rows, :] * wave_ref[0, 0, rows, :]).astype(jnp.bfloat16)
        joined[rows, width:] = (ratio[rows, :] * wave_ref[0, 1, rows, :]).astype(jnp.bfloat16)
        return carry

    lax.fori_loop(0, width // tile, fix, 0)

    def emit(rows, real, imag):
        obj_re = patch_ref[0, rows, :].astype(jnp.float32)
        obj_im = patch_ref[1, rows, :].astype(jnp.float32)
        diff_re = real - exit_ref[0, 0, rows, :].astype(jnp.float32)
        diff_im = imag - exit_ref[0, 1, rows, :].astype(jnp.float32)
        add_re = obj_re * diff_re + obj_im * diff_im
        add_im = obj_re * diff_im - obj_im * diff_re
        if grad_in is not None:
            add_re = grad_in[0, 0, rows, :] + add_re
            add_im = grad_in[0, 1, rows, :] + add_im
        grad_ref[0, 0, rows, :] = add_re
        grad_ref[0, 1, rows, :] = add_im

    transform(joined, stacked, minus, plus, emit)


def finish_kernel(mode, norm_ref, grad_ref, illum_ref, probe_ref, dir_ref, *rest):
    new_probe, new_dir, new_norm = rest[-4:-1]
    denom = rest[-1]
    width = illum_ref.shape[0]
    tile = 32
    steps = width // tile
    pixels = float(width * width)

    def rows_of(step):
        return pl.ds(pl.multiple_of(step * tile, tile), tile)

    def fold(block):
        return jnp.sum(block.reshape(tile // 8, 8, width), axis=0)

    zero = jnp.zeros((8, width), jnp.float32)
    total = jnp.sum(lax.fori_loop(0, steps, lambda i, acc: acc + fold(illum_ref[rows_of(i), :]), zero))
    shift = total / pixels

    def one(step, acc):
        rows = rows_of(step)
        den = illum_ref[rows, :] + shift
        g_re, g_im = grad_ref[0, 0, rows, :], grad_ref[0, 1, rows, :]
        p_re, p_im = g_re / den, g_im / den
        new_dir[0, 0, rows, :] = p_re
        new_dir[1, 0, rows, :] = p_im
        return acc + fold(g_re * p_re + g_im * p_im)

    norm = jnp.sum(lax.fori_loop(0, steps, one, zero)) / pixels
    new_norm[0, 0] = norm
    beta = norm / norm_ref[mode]

    def two(step, acc):
        rows = rows_of(step)
        upper, lower = acc
        d_re = new_dir[0, 0, rows, :] + beta * dir_ref[0, 0, rows, :]
        d_im = new_dir[1, 0, rows, :] + beta * dir_ref[1, 0, rows, :]
        new_dir[0, 0, rows, :] = d_re
        new_dir[1, 0, rows, :] = d_im
        upper = upper + fold(grad_ref[0, 0, rows, :] * d_re + grad_ref[0, 1, rows, :] * d_im)
        lower = lower + fold(illum_ref[rows, :] * (d_re * d_re + d_im * d_im))
        return (upper, lower)

    upper, lower = lax.fori_loop(0, steps, two, (zero, zero))
    alpha = (jnp.sum(upper) / pixels) / (jnp.sum(lower) / pixels + 1.0)

    def three(step, carry):
        rows = rows_of(step)
        new_probe[0, 0, rows, :] = probe_ref[0, 0, rows, :] + alpha * new_dir[0, 0, rows, :]
        new_probe[1, 0, rows, :] = probe_ref[1, 0, rows, :] + alpha * new_dir[1, 0, rows, :]
        return carry

    lax.fori_loop(0, steps, three, 0)


def whole(shape):
    return pl.BlockSpec(shape, lambda *_: (0,) * len(shape))


def table_scratch(width):
    return [
        pltpu.VMEM((2 * width, 2 * width), jnp.bfloat16),
        pltpu.VMEM((2 * width, 2 * width), jnp.bfloat16),
        pltpu.VMEM((width, 2 * width), jnp.bfloat16),
        pltpu.VMEM((2 * width, width), jnp.bfloat16),
    ]


def params():
    return pltpu.CompilerParams(dimension_semantics=("arbitrary",), vmem_limit_bytes=VMEM_LIMIT)


def cost(modes, width, moved):
    return pl.CostEstimate(flops=modes * 16 * width**3, bytes_accessed=moved, transcendentals=0)


def forward(base, probe, patch):
    modes, width = probe.shape[1], probe.shape[2]
    return pl.pallas_call(
        forward_kernel,
        grid=(modes,),
        in_specs=[
            whole(base.shape),
            pl.BlockSpec((2, 1, width, width), lambda m: (0, m, 0, 0)),
            whole(patch.shape),
        ],
        out_specs=[
            pl.BlockSpec((1, 2, width, width), lambda m: (m, 0, 0, 0)),
            pl.BlockSpec((1, 2, width, width), lambda m: (m, 0, 0, 0)),
            whole((width, width)),
        ],
        out_shape=[
            jax.ShapeDtypeStruct((modes, 2, width, width), jnp.float32),
            jax.ShapeDtypeStruct((modes, 2, width, width), jnp.bfloat16),
            jax.ShapeDtypeStruct((width, width), jnp.float32),
        ],
        scratch_shapes=table_scratch(width),
        compiler_params=params(),
        cost_estimate=cost(modes, width, modes * width * width * 20),
        name="forward",
    )(base, probe, patch)


def backward(base, total, amplitude, index, wave, exits, patch, grad, start, count):
    width = total.shape[0]
    at = lambda m: (m + start, 0, 0, 0)
    block = (1, 2, width, width)
    operands = [base, total, amplitude, wave, exits, patch]
    in_specs = [
        whole(base.shape),
        whole(total.shape),
        pl.BlockSpec((1, width, width), lambda m: (index, 0, 0)),
        pl.BlockSpec(block, at),
        pl.BlockSpec(block, at),
        whole(patch.shape),
    ]
    if grad is not None:
        operands.append(grad)
        in_specs.append(pl.BlockSpec(block, at))
    return pl.pallas_call(
        functools.partial(backward_kernel, grad is None),
        grid=(count,),
        in_specs=in_specs,
        out_specs=pl.BlockSpec(block, lambda m: (m, 0, 0, 0)),
        out_shape=jax.ShapeDtypeStruct((count, 2, width, width), jnp.float32),
        scratch_shapes=table_scratch(width) + [pltpu.VMEM((width, width), jnp.float32)],
        compiler_params=params(),
        cost_estimate=cost(count, width, count * width * width * 24),
        name="backward",
    )(*operands)


def finish(mode, prev_norm, grad, illum, probe, direction, outs):
    width = illum.shape[0]
    block = pl.BlockSpec((2, 1, width, width), lambda m: (0, mode, 0, 0))
    operands = [prev_norm, grad, illum, probe, direction]
    in_specs = [
        pl.BlockSpec(memory_space=pltpu.SMEM),
        whole(grad.shape),
        whole(illum.shape),
        block,
        block,
    ]
    aliases = {}
    if outs is not None:
        aliases = {len(operands): 0, len(operands) + 1: 1}
        operands += list(outs)
        in_specs += [pl.BlockSpec(memory_space=pl.ANY)] * 2
    return pl.pallas_call(
        functools.partial(finish_kernel, mode),
        grid=(1,),
        in_specs=in_specs,
        out_specs=[block, block, pl.BlockSpec(memory_space=pltpu.SMEM)],
        out_shape=[
            jax.ShapeDtypeStruct(probe.shape, jnp.float32),
            jax.ShapeDtypeStruct(probe.shape, jnp.float32),
            jax.ShapeDtypeStruct((1, 1), jnp.float32),
        ],
        scratch_shapes=[pltpu.VMEM((8, 128), jnp.float32)],
        input_output_aliases=aliases,
        compiler_params=params(),
        cost_estimate=pl.CostEstimate(flops=width * width * 30, bytes_accessed=width * width * 44, transcendentals=0),
        name="finish",
    )(*operands)


def on_device(probe, prev_direction, prev_norm, object_tile, offsets, amplitude):
    width = probe.shape[2]
    modes = probe.shape[1]
    positions = amplitude.shape[0]
    base = base_table(width)
    illum = jnp.zeros((width, width), jnp.float32)
    patches, kept = [], []
    for index in range(positions):
        patch = lax.dynamic_slice(
            object_tile, (jnp.int32(0), offsets[index, 0], offsets[index, 1]), (2, width, width)
        )
        patches.append(patch)
        wave, exits, local_sum = forward(base, probe, patch)
        if kept:
            local_sum, earlier = lax.optimization_barrier((local_sum, kept[-1][2]))
            kept[-1] = (kept[-1][0], kept[-1][1], earlier)
        total = lax.psum(local_sum, "mode")
        kept.append((wave, exits, total))
        wide = patch.astype(jnp.float32)
        illum = illum + wide[0] * wide[0] + wide[1] * wide[1]
    grad = None
    for index in range(positions - 1):
        wave, exits, total = kept[index]
        grad = backward(base, total, amplitude, index, wave, exits, patches[index], grad, 0, modes)
    wave, exits, total = kept[-1]
    sums = []
    for mode in range(modes):
        part = backward(base, total, amplitude, positions - 1, wave, exits, patches[-1], grad, mode, 1)
        if mode == 0:
            part, illum = lax.psum((part, illum), "grp")
        else:
            part, sums[-1] = lax.optimization_barrier((part, sums[-1]))
            part = lax.psum(part, "grp")
        sums.append(part)
    outs, norms = None, []
    for mode in range(modes):
        *outs, norm = finish(mode, prev_norm, sums[mode], illum, probe, prev_direction, outs)
        norms.append(norm.reshape(1))
    return (outs[0], outs[1], jnp.concatenate(norms))


def solution(mesh):
    return jax.shard_map(
        on_device,
        mesh=mesh,
        in_specs=(
            P(None, "mode", None, None),
            P(None, "mode", None, None),
            P("mode"),
            P(None, "grp", None),
            P("grp", None),
            P("grp", None, None),
        ),
        out_specs=(P(None, "mode", None, None), P(None, "mode", None, None), P("mode")),
        check_vma=False,
    )
```

time: 524 us -> 585 us (1.12); the launches traced: 514 us -> 584 us
  waiting for transfers between devices: 171 us -> 427 us
  local copies, waits for them, and re-layouts: 139 us -> 2.15 us
  Pallas kernels: 0 us -> 118 us
  other arithmetic: 108 us -> 14.8 us
  matrix products: 72.5 us -> 0 us
    psum x1 -> x6, waiting for transfers between devices: 166 us -> 427 us  [the longest x3 288 us: on_device(): part = lax.psum(part, 'grp')]
    pallas_call x0 -> x11, Pallas kernels: none -> 118 us  [the longest x5 54.4 us: backward(): pl.pallas_call(functools.partial(backward_kernel, grad is None), grid=(co...]
    unnamed x70 -> x2, local copies, waits for them, and re-layouts: 83.9 us -> 0.73 us
    dot_general x8 -> x0, matrix products: 72.5 us -> none  [the longest x4 38.8 us: transform(): half = jnp.dot(joined, right, preferred_element_type=jnp.float32)]
    slice x7 -> x0, local copies, waits for them, and re-layouts: 26.4 us -> none  [the longest x4 8.34 us: transform(): stacked = jnp.concatenate([half[:, :, :width], half[:, :, width:]], axis=1)]
    another operation x3 -> x1, other arithmetic: 25.8 us -> 1.08 us  [base_table(): return jnp.stack([real_part, imag_part])]
    convert_element_type x6 -> x2, other arithmetic: 28.1 us -> 7.54 us  [the longest x1 4.39 us: base_table(): imag_part = (jnp.sin(angle) * scale).astype(jnp.bfloat16)]
    reduce_sum x5 -> x0, other arithmetic: 19.7 us -> none  [the longest x1 8.56 us: finish(): upper = jnp.sum(grad_re * dir_re + grad_im * dir_im, axis=(1, 2))]
  transfers between devices with their start and end apart: 5 -> 6, of which waited for: 2 -> 6; matrix products, arithmetic and copies ran while one was open for 24% -> 1% of each run, Pallas kernels for 0% -> 11%
where the time goes in v1:
time: 585 us; the launch traced here: 584 us
  waiting for transfers between devices  427 us (73%)
  Pallas kernels  118 us (20%)
  between operations  21.9 us (4%)
  other arithmetic  14.8 us (3%)
    psum x3, waiting for transfers between devices, on_device(): part = lax.psum(part, 'grp')  288 us
    psum x1, waiting for transfers between devices, on_device(): part, illum = lax.psum((part, illum), 'grp')  89.3 us
    pallas_call x5, Pallas kernels, backward(): pl.pallas_call(functools.partial(backward_kernel, grad is None), grid=(co...  54.4 us
    psum x2, waiting for transfers between devices, on_device(): total = lax.psum(local_sum, 'mode')  49.1 us
    pallas_call x2, Pallas kernels, forward(): pl.pallas_call(forward_kernel, grid=(modes,), in_specs=[whole(base.shape)...  35.9 us
    pallas_call x4, Pallas kernels, finish(): pl.pallas_call(functools.partial(finish_kernel, mode), grid=(1,), in_spec...  28.2 us
  transfers between devices with their start and end apart: 6, of which 6 were waited for; matrix products, arithmetic and copies ran while one was open for 1% of the time, Pallas kernels for 11%

profile of v1, /device:TPU:0, one launch (start us, length us, event | category | flops | bytes accessed | tf_op | source)
XLA Modules:
  0.0 584.4 jit_solution(1998023207288754207)
XLA Ops:
  7.2 1.4 fusion.12
  13.8 4.4 multiply_convert_fusion
  20.8 1.1 pad_maximum_fusion.base_ref
  21.9 0.7 copy-done
  22.6 3.2 fusion.10
  25.7 18.0 %forward.3 = (f32[4,2,512,512]{3,2,1,0:T(8,128)}, bf16[4,2,512,512]{3,2,1,0:T(8,128)(2,1)}, f32[512,512]{1,0:T(8,128)}) custom-call(bf16[2,512,512]{2,1,0:T(8,128)(2,1)} %pad_maximum_fusion.base_ref, f32[2,4,512,512]{3,2,1,0:T(8,128)} %probe_ref.11, bf16[2,512,512]{2,1,0:T(8,128)(2,1)} %get-tuple-element.58.patch_ref), custom_call_target="tpu_custom_call" | custom-call | flops 8589934592 | bytes 20971520 | tf_op jit(solution)/shard_map/forward/pallas_call | solution.py:212
  43.8 18.0 %forward.2 = (f32[4,2,512,512]{3,2,1,0:T(8,128)}, bf16[4,2,512,512]{3,2,1,0:T(8,128)(2,1)}, f32[512,512]{1,0:T(8,128)}) custom-call(bf16[2,512,512]{2,1,0:T(8,128)(2,1)} %pad_maximum_fusion.base_ref, f32[2,4,512,512]{3,2,1,0:T(8,128)} %probe_ref.11, bf16[2,512,512]{2,1,0:T(8,128)(2,1)} %get-tuple-element.62.patch_ref), custom_call_target="tpu_custom_call" | custom-call | flops 8589934592 | bytes 20971520 | tf_op jit(solution)/shard_map/forward/pallas_call | solution.py:212
  61.7 25.0 %all-reduce.8.cloned.1.call-done.total_ref = f32[512,512]{1,0:T(8,128)} async-done(((f32[512,512]{1,0:T(8,128)}), f32[512,512]{1,0:T(8,128)}) %all-reduce.8.cloned.1.call-update) | async-done | bytes 1048592 | tf_op jit(solution)/shard_map/psum | solution.py:316
  86.7 18.2 %backward.5.rest_0_ = f32[4,2,512,512]{3,2,1,0:T(8,128)} custom-call(bf16[2,512,512]{2,1,0:T(8,128)(2,1)} %pad_maximum_fusion.base_ref, f32[512,512]{1,0:T(8,128)} %all-reduce.8.cloned.1.call-done.total_ref, bf16[2,512,512]{2,1,0:T(8,128)(2,1)} %amp_ref.9, f32[4,2,512,512]{3,2,1,0:T(8,128)} %get-tuple-element.35.wave_ref, ...), custom_call_target="tpu_custom_call" | custom-call | flops 8589934592 | bytes 25165824 | tf_op jit(solution)/shard_map/backward/pallas_call | solution.py:253
  105.0 24.1 %all-reduce.10.cloned.1.call-done.total_ref = f32[512,512]{1,0:T(8,128)} async-done(((f32[512,512]{1,0:T(8,128)}), f32[512,512]{1,0:T(8,128)}) %all-reduce.10.cloned.1.call-update) | async-done | bytes 1048592 | tf_op jit(solution)/shard_map/psum | solution.py:316
  129.1 9.0 %backward.9 = f32[1,2,512,512]{3,2,1,0:T(8,128)} custom-call(bf16[2,512,512]{2,1,0:T(8,128)(2,1)} %pad_maximum_fusion.base_ref, f32[512,512]{1,0:T(8,128)} %all-reduce.10.cloned.1.call-done.total_ref, bf16[2,512,512]{2,1,0:T(8,128)(2,1)} %amp_ref.9, f32[4,2,512,512]{3,2,1,0:T(8,128)} %get-tuple-element.32.wave_ref, ...), custom_call_target="tpu_custom_call" | custom-call | flops 2147483648 | bytes 6291456 | tf_op jit(solution)/shard_map/backward/pallas_call | solution.py:253
  138.2 9.0 %backward.8 = f32[1,2,512,512]{3,2,1,0:T(8,128)} custom-call(bf16[2,512,512]{2,1,0:T(8,128)(2,1)} %pad_maximum_fusion.base_ref, f32[512,512]{1,0:T(8,128)} %all-reduce.10.cloned.1.call-done.total_ref, bf16[2,512,512]{2,1,0:T(8,128)(2,1)} %amp_ref.9, f32[4,2,512,512]{3,2,1,0:T(8,128)} %get-tuple-element.32.wave_ref, ...), custom_call_target="tpu_custom_call" | custom-call | flops 2147483648 | bytes 6291456 | tf_op jit(solution)/shard_map/backward/pallas_call | solution.py:253
  147.2 89.3 %all-reduce.12.cloned.1.call-done.grad_ref = f32[1,2,512,512]{3,2,1,0:T(8,128)} async-done(((f32[1,2,512,512]{3,2,1,0:T(8,128)}), f32[1,2,512,512]{3,2,1,0:T(8,128)}) %all-reduce.12.cloned.1.call-update) | async-done | bytes 2097168 | tf_op jit(solution)/shard_map/psum | solution.py:329
  236.6 9.0 %backward.7 = f32[1,2,512,512]{3,2,1,0:T(8,128)} custom-call(bf16[2,512,512]{2,1,0:T(8,128)(2,1)} %pad_maximum_fusion.base_ref, f32[512,512]{1,0:T(8,128)} %all-reduce.10.cloned.1.call-done.total_ref, bf16[2,512,512]{2,1,0:T(8,128)(2,1)} %amp_ref.9, f32[4,2,512,512]{3,2,1,0:T(8,128)} %get-tuple-element.32.wave_ref, ...), custom_call_target="tpu_custom_call" | custom-call | flops 2147483648 | bytes 6291456 | tf_op jit(solution)/shard_map/backward/pallas_call | solution.py:253
  245.7 92.3 %all-reduce.14.cloned.1.call-done.grad_ref = f32[1,2,512,512]{3,2,1,0:T(8,128)} async-done(((f32[1,2,512,512]{3,2,1,0:T(8,128)}), f32[1,2,512,512]{3,2,1,0:T(8,128)}) %all-reduce.14.cloned.1.call-update) | async-done | bytes 2097168 | tf_op jit(solution)/shard_map/psum | solution.py:332
  338.2 3.0 fusion.4
  341.2 9.0 %backward.6 = f32[1,2,512,512]{3,2,1,0:T(8,128)} custom-call(bf16[2,512,512]{2,1,0:T(8,128)(2,1)} %pad_maximum_fusion.base_ref, f32[512,512]{1,0:T(8,128)} %all-reduce.10.cloned.1.call-done.total_ref, bf16[2,512,512]{2,1,0:T(8,128)(2,1)} %amp_ref.9, f32[4,2,512,512]{3,2,1,0:T(8,128)} %get-tuple-element.32.wave_ref, ...), custom_call_target="tpu_custom_call" | custom-call | flops 2147483648 | bytes 6291456 | tf_op jit(solution)/shard_map/backward/pallas_call | solution.py:253
  350.3 88.5 %all-reduce.16.cloned.1.call-done.grad_ref = f32[1,2,512,512]{3,2,1,0:T(8,128)} async-done(((f32[1,2,512,512]{3,2,1,0:T(8,128)}), f32[1,2,512,512]{3,2,1,0:T(8,128)}) %all-reduce.16.cloned.1.call-update) | async-done | bytes 2097168 | tf_op jit(solution)/shard_map/psum | solution.py:332
  438.8 107.3 %all-reduce.18.cloned.1.call-done = (f32[1,2,512,512]{3,2,1,0:T(8,128)}, f32[512,512]{1,0:T(8,128)}) async-done(((f32[1,2,512,512]{3,2,1,0:T(8,128)}, f32[512,512]{1,0:T(8,128)}), (f32[1,2,512,512]{3,2,1,0:T(8,128)}, f32[512,512]{1,0:T(8,128)})) %all-reduce.18.cloned.1.call-update) | async-done | bytes 3145744 | tf_op jit(solution)/shard_map/psum | solution.py:332
  546.2 7.0 %finish.4 = (f32[2,4,512,512]{3,2,1,0:T(8,128)}, f32[2,4,512,512]{3,2,1,0:T(8,128)}, f32[1,1]{1,0:T(1,128)}) custom-call(f32[4]{0:T(128)} %norm_ref.7, f32[1,2,512,512]{3,2,1,0:T(8,128)} %all-reduce.12.cloned.1.call-done.grad_ref, f32[512,512]{1,0:T(8,128)} %get-tuple-element.56.illum_ref, f32[2,4,512,512]{3,2,1,0:T(8,128)} %probe_ref.11, ...), custom_call_target="tpu_custom_call" | custom-call | flops 7864320 | bytes 11534336 | tf_op jit(solution)/shard_map/finish/pallas_call | solution.py:282
  553.2 7.0 %finish.5 = (f32[2,4,512,512]{3,2,1,0:T(8,128)}, f32[2,4,512,512]{3,2,1,0:T(8,128)}, f32[1,1]{1,0:T(1,128)}) custom-call(f32[4]{0:T(128)} %norm_ref.7, f32[1,2,512,512]{3,2,1,0:T(8,128)} %all-reduce.14.cloned.1.call-done.grad_ref, f32[512,512]{1,0:T(8,128)} %get-tuple-element.56.illum_ref, ...), custom_call_target="tpu_custom_call", output_to_operand_aliasing={{0}: (5, {}), {1}: (6, {})} | custom-call | flops 7864320 | bytes 11534336 | tf_op jit(solution)/shard_map/finish/pallas_call | solution.py:282
  560.3 7.0 %finish.6 = (f32[2,4,512,512]{3,2,1,0:T(8,128)}, f32[2,4,512,512]{3,2,1,0:T(8,128)}, f32[1,1]{1,0:T(1,128)}) custom-call(f32[4]{0:T(128)} %norm_ref.7, f32[1,2,512,512]{3,2,1,0:T(8,128)} %all-reduce.16.cloned.1.call-done.grad_ref, f32[512,512]{1,0:T(8,128)} %get-tuple-element.56.illum_ref, ...), custom_call_target="tpu_custom_call", output_to_operand_aliasing={{0}: (5, {}), {1}: (6, {})} | custom-call | flops 7864320 | bytes 11534336 | tf_op jit(solution)/shard_map/finish/pallas_call | solution.py:282
  567.3 7.0 %finish.7 = (f32[2,4,512,512]{3,2,1,0:T(8,128)}, f32[2,4,512,512]{3,2,1,0:T(8,128)}, f32[1,1]{1,0:T(1,128)}) custom-call(f32[4]{0:T(128)} %norm_ref.7, f32[1,2,512,512]{3,2,1,0:T(8,128)} %get-tuple-element.55.grad_ref, f32[512,512]{1,0:T(8,128)} %get-tuple-element.56.illum_ref, ...), custom_call_target="tpu_custom_call", output_to_operand_aliasing={{0}: (5, {}), {1}: (6, {})} | custom-call | flops 7864320 | bytes 11534336 | tf_op jit(solution)/shard_map/finish/pallas_call | solution.py:282
  574.4 3.2 pad_maximum_fusion.1
  (13 shorter events, 0.5 us)
Async XLA Ops:
  7.2 79.5 %all-reduce.8.cloned.1.call-start = ((), (), s32[]{:S(2)}) async-start(), calls=%async_computation | async-start | bytes 2097152 | tf_op jit(solution)/shard_map/psum | solution.py:316
  20.8 1.8 copy-start
  43.7 85.4 %all-reduce.10.cloned.1.call-start = ((), (), s32[]{:S(2)}) async-start(), calls=%async_computation.1 | async-start | bytes 2097152 | tf_op jit(solution)/shard_map/psum | solution.py:316
  86.7 149.8 %all-reduce.12.cloned.1.call-start = ((), (), s32[]{:S(2)}) async-start(), calls=%async_computation.2 | async-start | bytes 4194304 | tf_op jit(solution)/shard_map/psum | solution.py:329
  138.2 199.8 %all-reduce.14.cloned.1.call-start = ((), (), s32[]{:S(2)}) async-start(), calls=%async_computation.3 | async-start | bytes 4194304 | tf_op jit(solution)/shard_map/psum | solution.py:332
  236.6 202.2 %all-reduce.16.cloned.1.call-start = ((), (), s32[]{:S(2)}) async-start(), calls=%async_computation.4 | async-start | bytes 4194304 | tf_op jit(solution)/shard_map/psum | solution.py:332
  338.0 208.2 %all-reduce.18.cloned.1.call-start = ((), (), s32[]{:S(2)}) async-start(), calls=%async_computation.5 | async-start | bytes 6291456 | tf_op jit(solution)/shard_map/psum | solution.py:332
Sparse Core Ops, SparseCore 0:
  43.8 42.7 all-reduce.7
  89.0 40.1 all-reduce.9
  138.3 98.2 all-reduce.11
  240.5 97.3 all-reduce.13
  341.4 97.3 all-reduce.15
  442.9 103.2 all-reduce.17

commit v2 on v1

--- a/solution.py
+++ b/solution.py
@@ -132,9 +132,8 @@
     transform(joined, stacked, minus, plus, emit)
 
 
-def finish_kernel(mode, norm_ref, grad_ref, illum_ref, probe_ref, dir_ref, *rest):
-    new_probe, new_dir, new_norm = rest[-4:-1]
-    denom = rest[-1]
+def finish_kernel(norm_ref, grad_ref, illum_ref, probe_ref, dir_ref, new_probe, new_dir, new_norm):
+    mode = pl.program_id(0)
     width = illum_ref.shape[0]
     tile = 32
     steps = width // tile
@@ -160,7 +159,7 @@
         return acc + fold(g_re * p_re + g_im * p_im)
 
     norm = jnp.sum(lax.fori_loop(0, steps, one, zero)) / pixels
-    new_norm[0, 0] = norm
+    new_norm[mode] = norm
     beta = norm / norm_ref[mode]
 
     def two(step, acc):
@@ -263,38 +262,34 @@
     )(*operands)
 
 
-def finish(mode, prev_norm, grad, illum, probe, direction, outs):
-    width = illum.shape[0]
-    block = pl.BlockSpec((2, 1, width, width), lambda m: (0, mode, 0, 0))
-    operands = [prev_norm, grad, illum, probe, direction]
-    in_specs = [
-        pl.BlockSpec(memory_space=pltpu.SMEM),
-        whole(grad.shape),
-        whole(illum.shape),
-        block,
-        block,
-    ]
-    aliases = {}
-    if outs is not None:
-        aliases = {len(operands): 0, len(operands) + 1: 1}
-        operands += list(outs)
-        in_specs += [pl.BlockSpec(memory_space=pl.ANY)] * 2
+def finish(prev_norm, grad, illum, probe, direction):
+    modes, width = probe.shape[1], illum.shape[0]
+    block = pl.BlockSpec((2, 1, width, width), lambda m: (0, m, 0, 0))
     return pl.pallas_call(
-        functools.partial(finish_kernel, mode),
-        grid=(1,),
-        in_specs=in_specs,
+        finish_kernel,
+        grid=(modes,),
+        in_specs=[
+            pl.BlockSpec(memory_space=pltpu.SMEM),
+            pl.BlockSpec((1, 2, width, width), lambda m: (m, 0, 0, 0)),
+            whole(illum.shape),
+            block,
+            block,
+        ],
         out_specs=[block, block, pl.BlockSpec(memory_space=pltpu.SMEM)],
         out_shape=[
             jax.ShapeDtypeStruct(probe.shape, jnp.float32),
             jax.ShapeDtypeStruct(probe.shape, jnp.float32),
-            jax.ShapeDtypeStruct((1, 1), jnp.float32),
-        ],
-        scratch_shapes=[pltpu.VMEM((8, 128), jnp.float32)],
-        input_output_aliases=aliases,
+            jax.ShapeDtypeStruct((modes,), jnp.float32),
+        ],
         compiler_params=params(),
-        cost_estimate=pl.CostEstimate(flops=width * width * 30, bytes_accessed=width * width * 44, transcendentals=0),
         name="finish",
-    )(*operands)
+    )(prev_norm, grad, illum, probe, direction)
+
+
+def sum_over_modes(local_sum):
+    if lax.axis_size("mode") != 2:
+        return lax.psum(local_sum, "mode")
+    return local_sum + lax.ppermute(local_sum, "mode", [(0, 1), (1, 0)])
 
 
 def on_device(probe, prev_direction, prev_norm, object_tile, offsets, amplitude):
@@ -310,10 +305,7 @@
         )
         patches.append(patch)
         wave, exits, local_sum = forward(base, probe, patch)
-        if kept:
-            local_sum, earlier = lax.optimization_barrier((local_sum, kept[-1][2]))
-            kept[-1] = (kept[-1][0], kept[-1][1], earlier)
-        total = lax.psum(local_sum, "mode")
+        total = sum_over_modes(local_sum)
         kept.append((wave, exits, total))
         wide = patch.astype(jnp.float32)
         illum = illum + wide[0] * wide[0] + wide[1] * wide[1]
@@ -322,20 +314,9 @@
         wave, exits, total = kept[index]
         grad = backward(base, total, amplitude, index, wave, exits, patches[index], grad, 0, modes)
     wave, exits, total = kept[-1]
-    sums = []
-    for mode in range(modes):
-        part = backward(base, total, amplitude, positions - 1, wave, exits, patches[-1], grad, mode, 1)
-        if mode == 0:
-            part, illum = lax.psum((part, illum), "grp")
-        else:
-            part, sums[-1] = lax.optimization_barrier((part, sums[-1]))
-            part = lax.psum(part, "grp")
-        sums.append(part)
-    outs, norms = None, []
-    for mode in range(modes):
-        *outs, norm = finish(mode, prev_norm, sums[mode], illum, probe, prev_direction, outs)
-        norms.append(norm.reshape(1))
-    return (outs[0], outs[1], jnp.concatenate(norms))
+    part = backward(base, total, amplitude, positions - 1, wave, exits, patches[-1], grad, 0, modes)
+    part, illum = lax.psum((part, illum), "grp")
+    return tuple(finish(prev_norm, part, illum, probe, prev_direction))
 
 
 def solution(mesh):

time: 585 us -> 322 us (0.55)
  waiting for transfers between devices: 427 us -> 190 us
  Pallas kernels: 118 us -> 90.1 us
    psum x5 -> x0, waiting for transfers between devices: 337 us -> none  [the longest x3 288 us: on_device(): part = lax.psum(part, 'grp')]
    psum x1, waiting for transfers between devices: 89.3 us -> 186 us  [on_device(): part, illum = lax.psum((part, illum), 'grp')]
    pallas_call x5 -> x2, Pallas kernels: 54.4 us -> 37.7 us  [backward(): pl.pallas_call(functools.partial(backward_kernel, grad is None), grid=(co...]
    pallas_call x4 -> x1, Pallas kernels: 28.2 us -> 16.5 us  [finish(): pl.pallas_call(finish_kernel, grid=(modes,), in_specs=[pl.BlockSpec(memor...]
  transfers between devices with their start and end apart: 6 -> 3, of which waited for: 6 -> 3; matrix products, arithmetic and copies ran while one was open for 1% -> 2% of each run, Pallas kernels for 11% -> 11%
where the time goes in v2:
time: 322 us
  waiting for transfers between devices  190 us (59%)
  Pallas kernels  90.1 us (28%)
  between operations  21.8 us (7%)
  other arithmetic  15.4 us (5%)
    psum x1, waiting for transfers between devices, on_device(): part, illum = lax.psum((part, illum), 'grp')  186 us
    pallas_call x2, Pallas kernels, backward(): pl.pallas_call(functools.partial(backward_kernel, grad is None), grid=(co...  37.7 us
    pallas_call x2, Pallas kernels, forward(): pl.pallas_call(forward_kernel, grid=(modes,), in_specs=[whole(base.shape)...  35.8 us
    pallas_call x1, Pallas kernels, finish(): pl.pallas_call(finish_kernel, grid=(modes,), in_specs=[pl.BlockSpec(memor...  16.5 us
  transfers between devices with their start and end apart: 3, of which 3 were waited for; matrix products, arithmetic and copies ran while one was open for 2% of the time, Pallas kernels for 11%

profile of v2, /device:TPU:0, one launch (start us, length us, event | category | flops | bytes accessed | tf_op | source)
XLA Modules:
  0.0 322.2 jit_solution(16310647379972051351)
XLA Ops:
  7.2 0.0 copy-start
  7.2 0.0 all-reduce.3.cloned.1.call-start
  7.2 1.4 fusion.12
  13.8 4.4 %multiply_convert_fusion = (bf16[1,512,512]{2,1,0:T(8,128)(2,1)S(1)}, bf16[1,512,512]{2,1,0:T(8,128)(2,1)S(1)}) fusion(), kind=kLoop, calls=%fused_computation.15 | loop fusion | flops 4718592 | bytes 1048576 | tf_op jit(solution)/shard_map/convert_element_type | solution.py:21
  20.8 1.1 pad_maximum_fusion.base_ref
  21.9 0.0 copy-done
  21.9 3.1 fusion.10
  25.0 17.9 %forward.3 = (f32[4,2,512,512]{3,2,1,0:T(8,128)}, bf16[4,2,512,512]{3,2,1,0:T(8,128)(2,1)}, f32[512,512]{1,0:T(8,128)}) custom-call(bf16[2,512,512]{2,1,0:T(8,128)(2,1)} %pad_maximum_fusion.base_ref, f32[2,4,512,512]{3,2,1,0:T(8,128)} %probe_ref.5, bf16[2,512,512]{2,1,0:T(8,128)(2,1)} %get-tuple-element.18.patch_ref), custom_call_target="tpu_custom_call" | custom-call | flops 8589934592 | bytes 20971520 | tf_op jit(solution)/shard_map/forward/pallas_call | solution.py:211
  42.9 3.1 collective-permute-start.1
  46.0 17.9 %forward.2 = (f32[4,2,512,512]{3,2,1,0:T(8,128)}, bf16[4,2,512,512]{3,2,1,0:T(8,128)(2,1)}, f32[512,512]{1,0:T(8,128)}) custom-call(bf16[2,512,512]{2,1,0:T(8,128)(2,1)} %pad_maximum_fusion.base_ref, f32[2,4,512,512]{3,2,1,0:T(8,128)} %probe_ref.5, bf16[2,512,512]{2,1,0:T(8,128)(2,1)} %get-tuple-element.22.patch_ref), custom_call_target="tpu_custom_call" | custom-call | flops 8589934592 | bytes 20971520 | tf_op jit(solution)/shard_map/forward/pallas_call | solution.py:211
  63.9 0.0 copy-start.2
  63.9 0.1 collective-permute-start
  64.0 3.1 fusion.4
  67.1 3.2 collective-permute-done.1
  70.3 0.0 copy-done.2
  70.3 2.4 add.61.total_ref
  72.7 18.3 %backward.2.rest_0_ = f32[4,2,512,512]{3,2,1,0:T(8,128)} custom-call(bf16[2,512,512]{2,1,0:T(8,128)(2,1)} %pad_maximum_fusion.base_ref, f32[512,512]{1,0:T(8,128)} %add.61.total_ref, bf16[2,512,512]{2,1,0:T(8,128)(2,1)} %amp_ref.3, f32[4,2,512,512]{3,2,1,0:T(8,128)} %get-tuple-element.13.wave_ref, bf16[4,2,512,512]{3,2,1,0:T(8,128)(2,1)} %get-tuple-element.14.exit_ref, ...), custom_call_target="tpu_custom_call" | custom-call | flops 8589934592 | bytes 25165824 | tf_op jit(solution)/shard_map/backward/pallas_call | solution.py:252
  91.1 0.8 collective-permute-done
  91.9 0.0 copy-done.1
  91.9 1.3 add.58.total_ref
  93.1 19.4 %backward.3 = f32[4,2,512,512]{3,2,1,0:T(8,128)} custom-call(bf16[2,512,512]{2,1,0:T(8,128)(2,1)} %pad_maximum_fusion.base_ref, f32[512,512]{1,0:T(8,128)} %add.58.total_ref, bf16[2,512,512]{2,1,0:T(8,128)(2,1)} %amp_ref.3, f32[4,2,512,512]{3,2,1,0:T(8,128)} %get-tuple-element.10.wave_ref, bf16[4,2,512,512]{3,2,1,0:T(8,128)(2,1)} %get-tuple-element.11.exit_ref, ...), custom_call_target="tpu_custom_call" | custom-call | flops 8589934592 | bytes 25165824 | tf_op jit(solution)/shard_map/backward/pallas_call | solution.py:252
  112.6 0.0 all-reduce.3.cloned.1.call-update
  112.6 186.3 %all-reduce.3.cloned.1.call-done = (f32[4,2,512,512]{3,2,1,0:T(8,128)}, f32[512,512]{1,0:T(8,128)}) async-done(((f32[4,2,512,512]{3,2,1,0:T(8,128)}, f32[512,512]{1,0:T(8,128)}), (f32[4,2,512,512]{3,2,1,0:T(8,128)}, f32[512,512]{1,0:T(8,128)})) %all-reduce.3.cloned.1.call-update) | async-done | bytes 9437200 | tf_op jit(solution)/shard_map/psum | solution.py:318
  298.9 16.5 %finish.1 = (f32[2,4,512,512]{3,2,1,0:T(8,128)}, f32[2,4,512,512]{3,2,1,0:T(8,128)}, f32[4]{0:T(128)}) custom-call(f32[4]{0:T(128)} %norm_ref.1, f32[4,2,512,512]{3,2,1,0:T(8,128)} %get-tuple-element.15.grad_ref, f32[512,512]{1,0:T(8,128)} %get-tuple-element.16.illum_ref, f32[2,4,512,512]{3,2,1,0:T(8,128)} %probe_ref.5, f32[2,4,512,512]{3,2,1,0:T(8,128)} %dir_ref.1), custom_call_target="tpu_custom_call" | custom-call | tf_op jit(solution)/shard_map/finish/pallas_call | solution.py:268
  (1 shorter events, 0.0 us)
Async XLA Ops:
  7.2 14.7 %copy-start = (bf16[2,640,640]{2,1,0:T(8,128)(2,1)S(1)}, bf16[2,640,640]{2,1,0:T(8,128)(2,1)}, u32[]{:S(2)}) copy-start(bf16[2,640,640]{2,1,0:T(8,128)(2,1)} %param.9) | copy-start | bytes 4915204
  7.2 291.7 %all-reduce.3.cloned.1.call-start = ((), (), s32[]{:S(2)}) async-start(), calls=%async_computation | async-start | bytes 18874368 | tf_op jit(solution)/shard_map/psum | solution.py:318
  42.9 27.4 %collective-permute-start.1 = (f32[512,512]{1,0:T(8,128)}, f32[512,512]{1,0:T(8,128)}, u32[]{:S(2)}, u32[]{:S(2)}) collective-permute-start(f32[512,512]{1,0:T(8,128)} %get-tuple-element.12), channel_id=1, source_target_pairs={{0,1},{1,0},{2,3},{3,2},{4,5},{5,4},{6,7},{7,6},{8,9},{9,8},{10,11... | collective-permute-start | bytes 3145736 | tf_op jit(solution)/shard_map/ppermute | solution.py:292
  63.9 6.4 %copy-start.2 = (f32[512,512]{1,0:T(8,128)S(1)}, f32[512,512]{1,0:T(8,128)}, u32[]{:S(2)}) copy-start(f32[512,512]{1,0:T(8,128)} %get-tuple-element.12) | copy-start | bytes 3145732
  63.9 27.9 %collective-permute-start = (f32[512,512]{1,0:T(8,128)}, f32[512,512]{1,0:T(8,128)S(1)}, u32[]{:S(2)}, u32[]{:S(2)}) collective-permute-start(f32[512,512]{1,0:T(8,128)} %get-tuple-element.9), channel_id=1, source_target_pairs={{0,1},{1,0},{2,3},{3,2},{4,5},{5,4},{6,7},{7,6},{8,9},{9,8},{10,11... | collective-permute-start | bytes 3145736 | tf_op jit(solution)/shard_map/ppermute | solution.py:292
  72.7 19.1 %copy-start.1 = (f32[512,512]{1,0:T(8,128)S(1)}, f32[512,512]{1,0:T(8,128)}, u32[]{:S(2)}) copy-start(f32[512,512]{1,0:T(8,128)} %get-tuple-element.9) | copy-start | bytes 3145732
Sparse Core Ops, SparseCore 0:
  112.7 186.1 all-reduce.2
